TPU v7x, 32 devices: a whole 2x2x4 slice. The times are simulated.
32 devices in a mesh: sweep: 2 (over y), row: 4 (over z), col: 2 (over x), dp: 2 (over core).
Axes of the slice: x: 2, y: 2, z: 4, core: 2. Of those that a mesh axis runs over, the one named last changes fastest.
Arguments:
- token_ids: int32 [4096], P(('sweep', 'dp')), parts along dimension 0, may hold values from 0 to 15999
- sweep_index: int32 [4], P('sweep'), parts along dimension 0, may hold values from 0 to 7
- table: bfloat16 [16000, 4096], P('row', 'col'), may hold values from -6 to 6
- cotangent: bfloat16 [4096, 4096], P(('sweep', 'dp', 'row'), 'col'), parts along dimension 0, may hold values from -0.13183594 to 0.13183594
- gate_weight: bfloat16 [4096, 11008], P('col', 'row'), may hold values from -0.09375 to 0.09375
- up_weight: bfloat16 [4096, 11008], P('col', 'row'), may hold values from -0.09375 to 0.09375
- down_weight: bfloat16 [11008, 4096], P('row', 'col'), may hold values from -0.0546875 to 0.0546875
Outputs:
- grad_gate: float32 [8192, 11008], P(('sweep', 'col'), ('row', 'dp')), parts along dimension 0
- grad_up: float32 [8192, 11008], P(('sweep', 'col'), ('row', 'dp')), parts along dimension 0
- grad_down: float32 [22016, 4096], P(('sweep', 'row'), ('col', 'dp')), parts along dimension 0
There are 2 independent parts, one for each index of `sweep`. A program takes and returns all parts, laid end to end along the dimension named above; an argument that names none is the same for every part. Nothing has to cross between parts.
All inputs are finite; a program needn't handle non-finite values.
Results may differ from a plain program's by a relative error of at most 0.0062.
Values may be sent and summed in bfloat16 or wider, within the bound.
A program may use at most 256 MiB of HBM per device.

v0:
```python
import jax
import jax.numpy as jnp
from jax import lax
from jax.sharding import PartitionSpec as P


def contract_rows(left, right):
    return lax.dot_general(
        left, right, (((0,), (0,)), ((), ())), preferred_element_type=jnp.float32
    )


def contract_cols(left, right):
    return lax.dot_general(
        left, right, (((1,), (1,)), ((), ())), preferred_element_type=jnp.float32
    )


def local(token_ids, sweep_index, table, cotangent, gate_weight, up_weight, down_weight):
    k_input = sweep_index[0].astype(jnp.float32)
    k_output = sweep_index[1].astype(jnp.float32)
    in_mult = jnp.exp2(k_input / 2.0 - 1.5)
    out_mult = jnp.exp2(1.0 - k_output / 2.0)
    table_rows = table.shape[0]
    offset = token_ids - lax.axis_index("row") * table_rows
    inside = jnp.logical_and(offset >= 0, offset < table_rows)
    picked = jnp.take(table, jnp.clip(offset, 0, table_rows - 1), axis=0)
    looked = jnp.where(inside[:, None], picked, jnp.zeros((), jnp.bfloat16))
    embedded = lax.psum(looked, "row").astype(jnp.float32)
    scaled = (in_mult * embedded).astype(jnp.bfloat16)
    grads_rows = lax.all_gather(cotangent, "row", axis=0, tiled=True)
    width = gate_weight.shape[1]
    x_rows = scaled
    d_rows = grads_rows
    gate_part = jnp.dot(x_rows, gate_weight, preferred_element_type=jnp.float32)
    up_part = jnp.dot(x_rows, up_weight, preferred_element_type=jnp.float32)
    back_part = contract_cols(d_rows, down_weight)
    mixed = lax.psum_scatter(
        jnp.concatenate([gate_part, up_part, back_part], axis=1),
        "col",
        scatter_dimension=0,
        tiled=True,
    )
    gate = mixed[:, :width]
    up = mixed[:, width : 2 * width]
    back = mixed[:, 2 * width :]
    back = out_mult * back
    sig = jax.nn.sigmoid(gate)
    silu = gate * sig
    hidden = (silu * up).astype(jnp.bfloat16)
    d_gate = (back * up * sig * (1.0 + gate * (1.0 - sig))).astype(jnp.bfloat16)
    d_up = (back * silu).astype(jnp.bfloat16)
    x_rows = scaled
    d_rows = grads_rows
    acc_down = contract_rows(lax.all_gather(hidden, "col", axis=0, tiled=True), d_rows)
    acc_gate = contract_rows(x_rows, lax.all_gather(d_gate, "col", axis=0, tiled=True))
    acc_up = contract_rows(x_rows, lax.all_gather(d_up, "col", axis=0, tiled=True))
    acc_down, acc_gate, acc_up = (acc_down, acc_gate, acc_up)
    acc_down = out_mult * acc_down
    grad_gate, grad_up, grad_down = (
        lax.psum_scatter(acc_gate, "dp", scatter_dimension=1, tiled=True),
        lax.psum_scatter(acc_up, "dp", scatter_dimension=1, tiled=True),
        lax.psum_scatter(acc_down, "dp", scatter_dimension=1, tiled=True),
    )
    return (grad_gate, grad_up, grad_down)


def solution(mesh):
    return jax.shard_map(
        local,
        mesh=mesh,
        in_specs=(
            P(("sweep", "dp")),
            P("sweep"),
            P("row", "col"),
            P(("sweep", "dp", "row"), "col"),
            P("col", "row"),
            P("col", "row"),
            P("row", "col"),
        ),
        out_specs=(
            P(("sweep", "col"), ("row", "dp")),
            P(("sweep", "col"), ("row", "dp")),
            P(("sweep", "row"), ("col", "dp")),
        ),
        check_vma=False,
    )
```

profile of v0, /device:TPU:0, one launch (start us, length us, event | category | flops | bytes accessed | tf_op | source)
XLA Modules:
  0.0 1019.8 jit_solution(16046031713710483176)
XLA Ops:
  7.2 0.0 all-reduce.2.cloned.1.call-start
  7.2 0.7 compare_and_fusion.1
  7.9 0.7 fusion.5
  8.6 16.6 %gather_fusion = bf16[1024,2048]{1,0:T(8,128)(2,1)} fusion(bf16[4000,2048]{1,0:T(8,128)(2,1)} %param.9, s32[1024]{0:T(1024)S(1)} %fusion.5), kind=kCustom, calls=%fused_computation | custom fusion | bytes 8392704 | tf_op jit(solution)/shard_map/jit(_take)/gather | solution.py:27
  25.2 0.0 copy-start.2
  25.2 4.1 select_select_fusion
  29.3 0.0 slice-start
  29.3 0.0 all-reduce.2.cloned.1.call-update
  29.3 0.0 all-gather.5.cloned.1.call-start
  29.4 0.7 all-gather.5.cloned.1.call-update
  30.1 0.3 reduce-scatter.5.cloned.1.call-start
  30.4 0.0 copy-done.2
  30.4 0.6 fusion.6
  31.8 155.4 %all-reduce.2.cloned.1.call-done = bf16[1024,2048]{1,0:T(8,128)(2,1)} async-done(((bf16[1024,2048]{1,0:T(8,128)(2,1)}), bf16[1024,2048]{1,0:T(8,128)(2,1)}) %all-reduce.2.cloned.1.call-update) | async-done | bytes 4194320 | tf_op jit(solution)/shard_map/psum | solution.py:29
  187.2 0.0 slice-start.1
  187.2 0.0 slice-start.2
  187.2 0.0 copy-start.3
  187.2 17.7 %fusion.3 = f32[1024,2752]{0,1:T(8,128)} fusion(bf16[2048,2752]{0,1:T(8,128)(2,1)} %param.12, bf16[1024,2048]{1,0:T(8,128)(2,1)} %all-reduce.2.cloned.1.call-done, f32[]{:T(128)} %bitcast), kind=kOutput, calls=%fused_computation.13 | convolution fusion | flops 11549016064 | bytes 26738692 | tf_op jit(solution)/shard_map/dot_general | solution.py:36
  204.8 0.0 slice-done
  204.8 0.0 slice-done.1
  204.9 0.0 slice-done.2
  204.9 0.0 copy-done.3
  204.9 14.8 %fusion.4 = f32[1024,2752]{0,1:T(8,128)} fusion(bf16[2048,2752]{0,1:T(8,128)(2,1)S(1)} %bitcast.11, bf16[1024,2048]{1,0:T(8,128)(2,1)S(1)} %copy-done.3, f32[]{:T(128)} %bitcast), kind=kOutput, calls=%fused_computation.14 | convolution fusion | flops 11549016064 | bytes 26738692 | tf_op jit(solution)/shard_map/dot_general | solution.py:35
  219.7 48.8 %all-gather.5.cloned.1.call-done = bf16[1024,2048]{1,0:T(8,128)(2,1)} async-done(((bf16[256,2048]{1,0:T(8,128)(2,1)}), bf16[1024,2048]{1,0:T(8,128)(2,1)}) %all-gather.5.cloned.1.call-update) | async-done | bytes 4194320 | tf_op jit(solution)/shard_map/all_gather | solution.py:31
  268.5 0.0 copy-start
  268.5 0.0 copy-start.1
  268.5 18.3 %fusion.7 = f32[1024,2752]{0,1:T(8,128)} fusion(bf16[1024,2048]{1,0:T(8,128)(2,1)} %all-gather.5.cloned.1.call-done, bf16[2752,2048]{1,0:T(8,128)(2,1)} %param.13), kind=kOutput, calls=%fused_computation.20 | convolution fusion | flops 11542724608 | bytes 26738688 | tf_op jit(solution)/shard_map/dot_general | solution.py:14
  286.8 0.0 copy-done
  286.8 0.0 copy-done.1
  286.8 24.1 %pad_maximum_fusion = f32[1024,8256]{0,1:T(8,128)} fusion(f32[1024,2752]{0,1:T(8,128)} %fusion.7, f32[1024,2752]{0,1:T(8,128)S(1)} %copy-done, f32[1024,2752]{0,1:T(8,128)S(1)} %copy-done.1), kind=kLoop, calls=%fused_computation.1 | loop fusion | flops 16908288 | bytes 67633152 | tf_op jit(solution)/shard_map/concatenate | solution.py:39
  310.8 0.0 reduce-scatter.5.cloned.1.call-update
  310.9 0.0 all-gather.11.cloned.1.call-start
  311.6 369.6 %reduce-scatter.5.cloned.1.call-done = f32[512,8256]{0,1:T(8,128)} async-done(((f32[1024,8256]{0,1:T(8,128)}), f32[512,8256]{0,1:T(8,128)}) %reduce-scatter.5.cloned.1.call-update) | async-done | bytes 16908304 | tf_op jit(solution)/shard_map/reduce_scatter | solution.py:38
  681.3 10.8 %multiply_convert_fusion.1 = (bf16[512,2752]{0,1:T(8,128)(2,1)}, bf16[512,2752]{0,1:T(8,128)(2,1)}, bf16[512,2752]{0,1:T(8,128)(2,1)}) fusion(f32[512,8256]{0,1:T(8,128)} %reduce-scatter.5.cloned.1.call-done, f32[]{:T(128)} %bitcast.1), kind=kLoop, calls=%fused_computation.5 | loop fusion | flops 22544384 | bytes 25362436 | tf_op jit(solution)/shard_map/convert_element_type | solution.py:50
  692.1 0.0 all-gather.11.cloned.1.call-update
  692.1 0.0 all-gather.9.cloned.1.call-start
  692.2 0.5 all-gather.9.cloned.1.call-update
  692.7 0.0 all-gather.7.cloned.1.call-start
  692.8 0.5 all-gather.7.cloned.1.call-update
  693.3 0.0 reduce-scatter.11.cloned.1.call-start
  693.4 71.9 %all-gather.11.cloned.1.call-done = bf16[1024,2752]{0,1:T(8,128)(2,1)} async-done(((bf16[512,2752]{0,1:T(8,128)(2,1)}), bf16[1024,2752]{0,1:T(8,128)(2,1)}) %all-gather.11.cloned.1.call-update) | async-done | bytes 5636112 | tf_op jit(solution)/shard_map/all_gather | solution.py:55
  765.3 19.4 %convolution_multiply_fusion = f32[2752,2048]{1,0:T(8,128)} fusion(bf16[1024,2752]{0,1:T(8,128)(2,1)} %all-gather.11.cloned.1.call-done, bf16[1024,2048]{1,0:T(8,128)(2,1)} %all-gather.5.cloned.1.call-done, f32[]{:T(128)} %bitcast.1), kind=kOutput, calls=%fused_computation.2 | convolution fusion | flops 11548360704 | bytes 32374788 | tf_op jit(solution)/shard_map/dot_general | solution.py:8
  784.7 0.0 reduce-scatter.11.cloned.1.call-update
  784.7 0.0 reduce-scatter.9.cloned.1.call-start
  784.7 55.5 %all-gather.9.cloned.1.call-done = bf16[1024,2752]{0,1:T(8,128)(2,1)} async-done(((bf16[512,2752]{0,1:T(8,128)(2,1)}), bf16[1024,2752]{0,1:T(8,128)(2,1)}) %all-gather.9.cloned.1.call-update) | async-done | bytes 5636112 | tf_op jit(solution)/shard_map/all_gather | solution.py:57
  840.3 19.3 %fusion.2 = f32[2048,2752]{0,1:T(8,128)} fusion(bf16[1024,2752]{0,1:T(8,128)(2,1)} %all-gather.9.cloned.1.call-done, bf16[1024,2048]{1,0:T(8,128)(2,1)} %all-reduce.2.cloned.1.call-done, f32[]{:T(128)} %bitcast), kind=kOutput, calls=%fused_computation.12 | convolution fusion | flops 11549016064 | bytes 32374788 | tf_op jit(solution)/shard_map/dot_general | solution.py:8
  859.5 0.0 reduce-scatter.9.cloned.1.call-update
  859.5 0.0 reduce-scatter.7.cloned.1.call-start
  859.6 55.6 %all-gather.7.cloned.1.call-done = bf16[1024,2752]{0,1:T(8,128)(2,1)} async-done(((bf16[512,2752]{0,1:T(8,128)(2,1)}), bf16[1024,2752]{0,1:T(8,128)(2,1)}) %all-gather.7.cloned.1.call-update) | async-done | bytes 5636112 | tf_op jit(solution)/shard_map/all_gather | solution.py:56
  915.2 23.9 %fusion.1 = f32[2048,2752]{0,1:T(8,128)} fusion(bf16[1024,2752]{0,1:T(8,128)(2,1)} %all-gather.7.cloned.1.call-done, bf16[1024,2048]{1,0:T(8,128)(2,1)} %all-reduce.2.cloned.1.call-done, f32[]{:T(128)} %bitcast), kind=kOutput, calls=%fused_computation.11 | convolution fusion | flops 11549016064 | bytes 32374788 | tf_op jit(solution)/shard_map/dot_general | solution.py:8
  939.1 0.0 reduce-scatter.7.cloned.1.call-update
  939.2 7.7 reduce-scatter.11.cloned.1.call-done
  946.8 33.1 %reduce-scatter.9.cloned.1.call-done = f32[2048,1376]{0,1:T(8,128)} async-done(((f32[2048,2752]{0,1:T(8,128)}), f32[2048,1376]{0,1:T(8,128)}) %reduce-scatter.9.cloned.1.call-update) | async-done | bytes 11272208 | tf_op jit(solution)/shard_map/reduce_scatter | solution.py:62
  980.0 33.1 %reduce-scatter.7.cloned.1.call-done = f32[2048,1376]{0,1:T(8,128)} async-done(((f32[2048,2752]{0,1:T(8,128)}), f32[2048,1376]{0,1:T(8,128)}) %reduce-scatter.7.cloned.1.call-update) | async-done | bytes 11272208 | tf_op jit(solution)/shard_map/reduce_scatter | solution.py:61
  (1 shorter events, 0.0 us)
Async XLA Ops:
  7.2 180.0 %all-reduce.2.cloned.1.call-start = ((), (), s32[]{:S(2)}) async-start(), calls=%async_computation.4 | async-start | bytes 8388608 | tf_op jit(solution)/shard_map/psum | solution.py:29
  25.2 5.2 copy-start.2
  29.3 175.6 %slice-start = ((s8[11272192]{0:T(1024)(128)(4,1)}), s8[2883584]{0:T(1024)(128)(4,1)S(1)}, s32[]{:S(2)}) async-start(s8[11272192]{0:T(1024)(128)(4,1)} %bitcast.10), calls=%async_computation.13 | async-start | bytes 5767168
  29.3 239.2 %all-gather.5.cloned.1.call-start = ((), (), s32[]{:S(2)}) async-start(), calls=%async_computation.5 | async-start | bytes 5242880 | tf_op jit(solution)/shard_map/all_gather | solution.py:31
  30.1 651.2 %reduce-scatter.5.cloned.1.call-start = ((), (), s32[]{:S(2)}) async-start(), calls=%async_computation.6 | async-start | bytes 50724864 | tf_op jit(solution)/shard_map/reduce_scatter | solution.py:38
  187.2 17.7 %slice-start.1 = ((s8[11272192]{0:T(1024)(128)(4,1)}), s8[4194304]{0:T(1024)(128)(4,1)S(1)}, s32[]{:S(2)}) async-start(s8[11272192]{0:T(1024)(128)(4,1)} %bitcast.10), calls=%async_computation.14 | async-start | bytes 8388608
  187.2 17.7 %slice-start.2 = ((s8[11272192]{0:T(1024)(128)(4,1)}), s8[4194304]{0:T(1024)(128)(4,1)S(1)}, s32[]{:S(2)}) async-start(s8[11272192]{0:T(1024)(128)(4,1)} %bitcast.10), calls=%async_computation.15 | async-start | bytes 8388608
  187.2 17.7 %copy-start.3 = (bf16[1024,2048]{1,0:T(8,128)(2,1)S(1)}, bf16[1024,2048]{1,0:T(8,128)(2,1)}, u32[]{:S(2)}) copy-start(bf16[1024,2048]{1,0:T(8,128)(2,1)} %all-reduce.2.cloned.1.call-done) | copy-start | bytes 12582916
  268.5 18.3 %copy-start = (f32[1024,2752]{0,1:T(8,128)S(1)}, f32[1024,2752]{0,1:T(8,128)}, u32[]{:S(2)}) copy-start(f32[1024,2752]{0,1:T(8,128)} %fusion.3) | copy-start | bytes 33816580
  268.5 18.3 %copy-start.1 = (f32[1024,2752]{0,1:T(8,128)S(1)}, f32[1024,2752]{0,1:T(8,128)}, u32[]{:S(2)}) copy-start(f32[1024,2752]{0,1:T(8,128)} %fusion.4) | copy-start | bytes 33816580
  310.9 454.4 %all-gather.11.cloned.1.call-start = ((), (), s32[]{:S(2)}) async-start(), calls=%async_computation.11 | async-start | bytes 8454144 | tf_op jit(solution)/shard_map/all_gather | solution.py:55
  692.1 148.1 %all-gather.9.cloned.1.call-start = ((), (), s32[]{:S(2)}) async-start(), calls=%async_computation.9 | async-start | bytes 8454144 | tf_op jit(solution)/shard_map/all_gather | solution.py:57
  692.7 222.5 %all-gather.7.cloned.1.call-start = ((), (), s32[]{:S(2)}) async-start(), calls=%async_computation.7 | async-start | bytes 8454144 | tf_op jit(solution)/shard_map/all_gather | solution.py:56
  693.3 253.5 %reduce-scatter.11.cloned.1.call-start = ((), (), s32[]{:S(2)}) async-start(), calls=%async_computation.12 | async-start | bytes 33816576 | tf_op jit(solution)/shard_map/reduce_scatter | solution.py:63
  784.7 195.3 %reduce-scatter.9.cloned.1.call-start = ((), (), s32[]{:S(2)}) async-start(), calls=%async_computation.10 | async-start | bytes 33816576 | tf_op jit(solution)/shard_map/reduce_scatter | solution.py:62
  859.5 153.5 %reduce-scatter.7.cloned.1.call-start = ((), (), s32[]{:S(2)}) async-start(), calls=%async_computation.8 | async-start | bytes 33816576 | tf_op jit(solution)/shard_map/reduce_scatter | solution.py:61
Sparse Core Ops, SparseCore 0:
  29.4 157.6 all-reduce.1
  188.8 79.6 all-gather.4
  311.0 370.2 reduce-scatter.4
  692.3 72.9 all-gather.10
  767.3 72.9 all-gather.8
  842.2 72.9 all-gather.6
  918.1 28.6 reduce-scatter.10
  949.7 30.1 reduce-scatter.8
  982.9 30.1 reduce-scatter.6
where the time goes:
time: 1020 us
  waiting for transfers between devices  833 us (82%)
  matrix products  113 us (11%)
  other arithmetic  40.4 us (4%)
  local copies, waits for them, and re-layouts  17.2 us (2%)
  between operations  15.5 us (2%)
    reduce_scatter x1, waiting for transfers between devices, local(): lax.psum_scatter(jnp.concatenate([gate_part, up_part, back_part], axis=1)...  370 us
    psum x1, waiting for transfers between devices, local(): embedded = lax.psum(looked, 'row').astype(jnp.float32)  155 us
    all_gather x1, waiting for transfers between devices, local(): lax.all_gather(hidden, 'col', axis=0, tiled=True)  71.9 us
    dot_general x3, matrix products, contract_rows(): lax.dot_general(left, right, (((0,), (0,)), ((), ())), preferred_element_...  62.5 us
    all_gather x1, waiting for transfers between devices, local(): lax.all_gather(d_gate, 'col', axis=0, tiled=True)  55.6 us
    all_gather x1, waiting for transfers between devices, local(): lax.all_gather(d_up, 'col', axis=0, tiled=True)  55.5 us
    all_gather x1, waiting for transfers between devices, local(): grads_rows = lax.all_gather(cotangent, 'row', axis=0, tiled=True)  48.8 us
    reduce_scatter x1, waiting for transfers between devices, local(): lax.psum_scatter(acc_gate, 'dp', scatter_dimension=1, tiled=True)  33.1 us
  transfers between devices with their start and end apart: 9, of which 9 were waited for; matrix products, arithmetic and copies ran while one was open for 9% of the time, Pallas kernels for 0%

commit v1 on v0

--- a/solution.py
+++ b/solution.py
@@ -2,6 +2,11 @@
 import jax.numpy as jnp
 from jax import lax
 from jax.sharding import PartitionSpec as P
+
+
+def gather_and_add(x, axis):
+    parts = lax.all_gather(x, axis)
+    return jnp.sum(parts, axis=0)
 
 
 def contract_rows(left, right):
@@ -26,7 +31,7 @@
     inside = jnp.logical_and(offset >= 0, offset < table_rows)
     picked = jnp.take(table, jnp.clip(offset, 0, table_rows - 1), axis=0)
     looked = jnp.where(inside[:, None], picked, jnp.zeros((), jnp.bfloat16))
-    embedded = lax.psum(looked, "row").astype(jnp.float32)
+    embedded = gather_and_add(looked, "row").astype(jnp.float32)
     scaled = (in_mult * embedded).astype(jnp.bfloat16)
     grads_rows = lax.all_gather(cotangent, "row", axis=0, tiled=True)
     width = gate_weight.shape[1]

time: 1020 us -> 1160 us (1.14)
  waiting for transfers between devices: 833 us -> 959 us
  other arithmetic: 40.4 us -> 53.6 us
    all_gather x0 -> x1, waiting for transfers between devices: none -> 270 us  [gather_and_add(): parts = lax.all_gather(x, axis)]
    psum x1 -> x0, waiting for transfers between devices: 155 us -> none  [local(): embedded = lax.psum(looked, 'row').astype(jnp.float32)]
    all_gather x1, waiting for transfers between devices: 48.8 us -> 61.9 us  [local(): grads_rows = lax.all_gather(cotangent, 'row', axis=0, tiled=True)]
    reduce_sum x0 -> x1, other arithmetic: none -> 12.1 us  [gather_and_add(): return jnp.sum(parts, axis=0)]
where the time goes in v1:
time: 1160 us
  waiting for transfers between devices  959 us (83%)
  matrix products  113 us (10%)
  other arithmetic  53.6 us (5%)
  local copies, waits for them, and re-layouts  17.3 us (1%)
  between operations  15.6 us (1%)
    reduce_scatter x1, waiting for transfers between devices, local(): lax.psum_scatter(jnp.concatenate([gate_part, up_part, back_part], axis=1)...  369 us
    all_gather x1, waiting for transfers between devices, gather_and_add(): parts = lax.all_gather(x, axis)  270 us
    all_gather x1, waiting for transfers between devices, local(): lax.all_gather(hidden, 'col', axis=0, tiled=True)  71.9 us
    dot_general x3, matrix products, contract_rows(): lax.dot_general(left, right, (((0,), (0,)), ((), ())), preferred_element_...  62.5 us
    all_gather x1, waiting for transfers between devices, local(): grads_rows = lax.all_gather(cotangent, 'row', axis=0, tiled=True)  61.9 us
    all_gather x1, waiting for transfers between devices, local(): lax.all_gather(d_up, 'col', axis=0, tiled=True)  55.5 us
    all_gather x1, waiting for transfers between devices, local(): lax.all_gather(d_gate, 'col', axis=0, tiled=True)  55.1 us
    reduce_scatter x1, waiting for transfers between devices, local(): lax.psum_scatter(acc_gate, 'dp', scatter_dimension=1, tiled=True)  33.1 us
  transfers between devices with their start and end apart: 9, of which 9 were waited for; matrix products, arithmetic and copies ran while one was open for 9% of the time, Pallas kernels for 0%

profile of v1, /device:TPU:0, one launch (start us, length us, event | category | flops | bytes accessed | tf_op | source)
XLA Modules:
  0.0 1159.8 jit_solution(1971199205998837749)
XLA Ops:
  7.2 0.0 all-gather.8.cloned.1.call-start
  7.2 0.7 all-gather.8.cloned.1.call-update
  7.9 0.0 all-gather.6.cloned.1.call-start
  8.0 0.7 fusion.6
  8.6 0.0 copy-start.1
  8.7 16.6 %gather_fusion = bf16[1024,2048]{1,0:T(8,128)(2,1)} fusion(bf16[4000,2048]{1,0:T(8,128)(2,1)} %param.9, s32[1024]{0:T(1024)S(1)} %fusion.6), kind=kCustom, calls=%fused_computation | custom fusion | bytes 8392704 | tf_op jit(solution)/shard_map/jit(_take)/gather | solution.py:32
  25.2 0.0 copy-done.1
  25.3 0.0 copy-start.2
  25.3 4.1 fusion.1
  29.4 0.0 all-gather.6.cloned.1.call-update
  29.4 0.3 reduce-scatter.5.cloned.1.call-start
  29.7 0.0 copy-done.2
  29.8 0.6 fusion.7
  31.1 61.9 %all-gather.8.cloned.1.call-done = bf16[1024,2048]{1,0:T(8,128)(2,1)} async-done(((bf16[256,2048]{1,0:T(8,128)(2,1)}), bf16[1024,2048]{1,0:T(8,128)(2,1)}) %all-gather.8.cloned.1.call-update) | async-done | bytes 4194320 | tf_op jit(solution)/shard_map/all_gather | solution.py:36
  93.0 17.5 %fusion.8 = f32[1024,2752]{0,1:T(8,128)} fusion(bf16[1024,2048]{1,0:T(8,128)(2,1)} %all-gather.8.cloned.1.call-done, bf16[2752,2048]{1,0:T(8,128)(2,1)} %param.13), kind=kOutput, calls=%fused_computation.21 | convolution fusion | flops 11542724608 | bytes 26738688 | tf_op jit(solution)/shard_map/dot_general | solution.py:19
  110.5 269.9 %all-gather.6.cloned.1.call-done = bf16[4,1024,2048]{2,1,0:T(8,128)(2,1)} async-done(((bf16[1,1024,2048]{2,1,0:T(8,128)(2,1)}), bf16[4,1024,2048]{2,1,0:T(8,128)(2,1)}) %all-gather.6.cloned.1.call-update) | async-done | bytes 16777232 | tf_op jit(solution)/shard_map/all_gather | solution.py:8
  380.5 12.1 %reduce_sum.12 = bf16[1024,2048]{1,0:T(8,128)(2,1)} reduce(bf16[4,1024,2048]{2,1,0:T(8,128)(2,1)} %all-gather.6.cloned.1.call-done, bf16[]{:T(256)} %constant.46.clone.1), dimensions={0}, to_apply=%region_0.1 | reduce | flops 6291456 | bytes 20971522 | tf_op jit(solution)/shard_map/reduce_sum | solution.py:9
  392.6 0.0 copy-start
  392.6 0.0 slice-start
  392.6 0.0 slice-start.1
  392.6 16.1 %fusion.4 = f32[1024,2752]{0,1:T(8,128)S(1)} fusion(bf16[2048,2752]{0,1:T(8,128)(2,1)} %param.12, bf16[1024,2048]{1,0:T(8,128)(2,1)} %reduce_sum.12, f32[]{:T(128)} %bitcast), kind=kOutput, calls=%fused_computation.14 | convolution fusion | flops 11549016064 | bytes 26738692 | tf_op jit(solution)/shard_map/dot_general | solution.py:41
  408.7 0.0 copy-done
  408.7 0.0 slice-start.2
  408.7 17.1 %fusion.5 = f32[1024,2752]{0,1:T(8,128)} fusion(bf16[2048,2752]{0,1:T(8,128)(2,1)} %param.11, bf16[1024,2048]{1,0:T(8,128)(2,1)S(1)} %copy-done, f32[]{:T(128)} %bitcast), kind=kOutput, calls=%fused_computation.15 | convolution fusion | flops 11549016064 | bytes 26738692 | tf_op jit(solution)/shard_map/dot_general | solution.py:40
  425.8 0.0 slice-done
  425.8 0.0 slice-done.1
  425.8 0.0 slice-done.2
  425.8 25.9 %pad_maximum_fusion = f32[1024,8256]{0,1:T(8,128)} fusion(f32[1024,2752]{0,1:T(8,128)S(1)} %bitcast.15, f32[1024,2752]{0,1:T(8,128)S(1)} %fusion.4, f32[1024,2752]{0,1:T(8,128)} %fusion.5), kind=kLoop, calls=%fused_computation.1 | loop fusion | flops 16908288 | bytes 67633152 | tf_op jit(solution)/shard_map/concatenate | solution.py:44
  451.7 0.0 reduce-scatter.5.cloned.1.call-update
  451.7 0.0 all-gather.14.cloned.1.call-start
  452.5 369.4 %reduce-scatter.5.cloned.1.call-done = f32[512,8256]{0,1:T(8,128)} async-done(((f32[1024,8256]{0,1:T(8,128)}), f32[512,8256]{0,1:T(8,128)}) %reduce-scatter.5.cloned.1.call-update) | async-done | bytes 16908304 | tf_op jit(solution)/shard_map/reduce_scatter | solution.py:43
  821.8 10.8 multiply_convert_fusion.1
  832.7 0.0 all-gather.14.cloned.1.call-update
  832.7 0.0 all-gather.12.cloned.1.call-start
  832.7 0.5 all-gather.12.cloned.1.call-update
  833.3 0.0 all-gather.10.cloned.1.call-start
  833.3 0.5 all-gather.10.cloned.1.call-update
  833.8 0.0 reduce-scatter.11.cloned.1.call-start
  833.9 71.9 %all-gather.14.cloned.1.call-done = bf16[1024,2752]{0,1:T(8,128)(2,1)} async-done(((bf16[512,2752]{0,1:T(8,128)(2,1)}), bf16[1024,2752]{0,1:T(8,128)(2,1)}) %all-gather.14.cloned.1.call-update) | async-done | bytes 5636112 | tf_op jit(solution)/shard_map/all_gather | solution.py:60
  905.8 19.4 %convolution_multiply_fusion = f32[2752,2048]{1,0:T(8,128)} fusion(bf16[1024,2752]{0,1:T(8,128)(2,1)} %all-gather.14.cloned.1.call-done, bf16[1024,2048]{1,0:T(8,128)(2,1)} %all-gather.8.cloned.1.call-done, f32[]{:T(128)} %bitcast.2), kind=kOutput, calls=%fused_computation.2 | convolution fusion | flops 11548360704 | bytes 32374788 | tf_op jit(solution)/shard_map/dot_general | solution.py:13
  925.2 0.0 reduce-scatter.11.cloned.1.call-update
  925.2 0.0 reduce-scatter.9.cloned.1.call-start
  925.2 55.5 %all-gather.12.cloned.1.call-done = bf16[1024,2752]{0,1:T(8,128)(2,1)} async-done(((bf16[512,2752]{0,1:T(8,128)(2,1)}), bf16[1024,2752]{0,1:T(8,128)(2,1)}) %all-gather.12.cloned.1.call-update) | async-done | bytes 5636112 | tf_op jit(solution)/shard_map/all_gather | solution.py:62
  980.8 19.2 %fusion.3 = f32[2048,2752]{0,1:T(8,128)} fusion(bf16[1024,2752]{0,1:T(8,128)(2,1)} %all-gather.12.cloned.1.call-done, bf16[1024,2048]{1,0:T(8,128)(2,1)} %reduce_sum.12, f32[]{:T(128)} %bitcast), kind=kOutput, calls=%fused_computation.13 | convolution fusion | flops 11549016064 | bytes 32374788 | tf_op jit(solution)/shard_map/dot_general | solution.py:13
  1000.0 0.0 reduce-scatter.9.cloned.1.call-update
  1000.0 0.0 reduce-scatter.7.cloned.1.call-start
  1000.1 55.1 %all-gather.10.cloned.1.call-done = bf16[1024,2752]{0,1:T(8,128)(2,1)} async-done(((bf16[512,2752]{0,1:T(8,128)(2,1)}), bf16[1024,2752]{0,1:T(8,128)(2,1)}) %all-gather.10.cloned.1.call-update) | async-done | bytes 5636112 | tf_op jit(solution)/shard_map/all_gather | solution.py:61
  1055.2 23.9 %fusion.2 = f32[2048,2752]{0,1:T(8,128)} fusion(bf16[1024,2752]{0,1:T(8,128)(2,1)} %all-gather.10.cloned.1.call-done, bf16[1024,2048]{1,0:T(8,128)(2,1)} %reduce_sum.12, f32[]{:T(128)} %bitcast), kind=kOutput, calls=%fused_computation.12 | convolution fusion | flops 11549016064 | bytes 32374788 | tf_op jit(solution)/shard_map/dot_general | solution.py:13
  1079.1 0.0 reduce-scatter.7.cloned.1.call-update
  1079.1 7.7 reduce-scatter.11.cloned.1.call-done
  1086.8 33.1 %reduce-scatter.9.cloned.1.call-done = f32[2048,1376]{0,1:T(8,128)} async-done(((f32[2048,2752]{0,1:T(8,128)}), f32[2048,1376]{0,1:T(8,128)}) %reduce-scatter.9.cloned.1.call-update) | async-done | bytes 11272208 | tf_op jit(solution)/shard_map/reduce_scatter | solution.py:67
  1119.9 33.1 %reduce-scatter.7.cloned.1.call-done = f32[2048,1376]{0,1:T(8,128)} async-done(((f32[2048,2752]{0,1:T(8,128)}), f32[2048,1376]{0,1:T(8,128)}) %reduce-scatter.7.cloned.1.call-update) | async-done | bytes 11272208 | tf_op jit(solution)/shard_map/reduce_scatter | solution.py:66
  (2 shorter events, 0.0 us)
Async XLA Ops:
  7.2 85.9 %all-gather.8.cloned.1.call-start = ((), (), s32[]{:S(2)}) async-start(), calls=%async_computation.5 | async-start | bytes 5242880 | tf_op jit(solution)/shard_map/all_gather | solution.py:36
  7.9 372.6 %all-gather.6.cloned.1.call-start = ((), (), s32[]{:S(2)}) async-start(), calls=%async_computation.4 | async-start | bytes 20971520 | tf_op jit(solution)/shard_map/all_gather | solution.py:8
  8.6 16.6 %copy-start.1 = (s32[1024]{0:T(1024)S(1)}, s32[1024]{0:T(1024)}, u32[]{:S(2)}) copy-start(s32[1024]{0:T(1024)} %param.7) | copy-start | bytes 12292
  25.3 4.5 copy-start.2
  29.4 792.4 %reduce-scatter.5.cloned.1.call-start = ((), (), s32[]{:S(2)}) async-start(), calls=%async_computation.6 | async-start | bytes 50724864 | tf_op jit(solution)/shard_map/reduce_scatter | solution.py:43
  392.6 16.1 %copy-start = (bf16[1024,2048]{1,0:T(8,128)(2,1)S(1)}, bf16[1024,2048]{1,0:T(8,128)(2,1)}, u32[]{:S(2)}) copy-start(bf16[1024,2048]{1,0:T(8,128)(2,1)} %reduce_sum.12) | copy-start | bytes 12582916
  392.6 33.2 %slice-start = ((s8[11272192]{0:T(1024)(128)(4,1)}), s8[4194304]{0:T(1024)(128)(4,1)S(1)}, s32[]{:S(2)}) async-start(s8[11272192]{0:T(1024)(128)(4,1)} %bitcast.14), calls=%async_computation.13 | async-start | bytes 8388608
  392.6 33.2 %slice-start.1 = ((s8[11272192]{0:T(1024)(128)(4,1)}), s8[4194304]{0:T(1024)(128)(4,1)S(1)}, s32[]{:S(2)}) async-start(s8[11272192]{0:T(1024)(128)(4,1)} %bitcast.14), calls=%async_computation.14 | async-start | bytes 8388608
  408.7 17.1 %slice-start.2 = ((s8[11272192]{0:T(1024)(128)(4,1)}), s8[2883584]{0:T(1024)(128)(4,1)S(1)}, s32[]{:S(2)}) async-start(s8[11272192]{0:T(1024)(128)(4,1)} %bitcast.14), calls=%async_computation.15 | async-start | bytes 5767168
  451.7 454.1 %all-gather.14.cloned.1.call-start = ((), (), s32[]{:S(2)}) async-start(), calls=%async_computation.11 | async-start | bytes 8454144 | tf_op jit(solution)/shard_map/all_gather | solution.py:60
  832.7 148.1 %all-gather.12.cloned.1.call-start = ((), (), s32[]{:S(2)}) async-start(), calls=%async_computation.9 | async-start | bytes 8454144 | tf_op jit(solution)/shard_map/all_gather | solution.py:62
  833.3 221.9 %all-gather.10.cloned.1.call-start = ((), (), s32[]{:S(2)}) async-start(), calls=%async_computation.7 | async-start | bytes 8454144 | tf_op jit(solution)/shard_map/all_gather | solution.py:61
  833.8 252.9 %reduce-scatter.11.cloned.1.call-start = ((), (), s32[]{:S(2)}) async-start(), calls=%async_computation.12 | async-start | bytes 33816576 | tf_op jit(solution)/shard_map/reduce_scatter | solution.py:68
  925.2 194.7 %reduce-scatter.9.cloned.1.call-start = ((), (), s32[]{:S(2)}) async-start(), calls=%async_computation.10 | async-start | bytes 33816576 | tf_op jit(solution)/shard_map/reduce_scatter | solution.py:67
  1000.0 153.0 %reduce-scatter.7.cloned.1.call-start = ((), (), s32[]{:S(2)}) async-start(), calls=%async_computation.8 | async-start | bytes 33816576 | tf_op jit(solution)/shard_map/reduce_scatter | solution.py:66
Sparse Core Ops, SparseCore 0:
  9.5 83.4 all-gather.7
  95.2 285.2 all-gather.5
  451.8 369.9 reduce-scatter.4
  832.8 72.9 all-gather.13
  907.8 72.9 all-gather.11
  982.2 72.9 all-gather.9
  1058.1 28.6 reduce-scatter.10
  1089.7 30.1 reduce-scatter.8
  1122.8 30.1 reduce-scatter.6
